TPU v7x, 256 devices: a whole 4x4x8 slice. The times are simulated.
256 devices in a mesh: samp: 4 (over z_hi, core), snp: 64 (over y, z_lo, x).
Axes of the slice: x: 4, y: 4, z: 8 (z_hi: 2, z_lo: 4; z = z_hi * 4 + z_lo), core: 2. Of those that a mesh axis runs over, the one named last changes fastest.
Arguments:
- genotypes: float32 [4096, 65536], P('samp', 'snp'), may hold values from -1 to 2, as said below
Outputs:
- band_r: float32 [65536, 4096], P('snp', 'samp')
Inputs may be any that keep to these rules, and one draw needn't show every extreme that they name: `genotypes`: -1 marks a missing dosage; every other value lies between 0 and 2. Every eighth sample (samples 0, 8, 16, ...) has no missing dosage, and over those samples each SNP's dosages run through 0, 1, 2 cyclically from a SNP's own starting value.
All inputs are finite; a program needn't handle non-finite values.
Results may differ from a plain program's by a relative error of at most 0.006.
Values may be sent and summed in bfloat16 or wider, within the bound.
A program may use at most 64 MiB of HBM per device.

v0:
```python
import jax
import jax.numpy as jnp
from jax import lax
from jax.sharding import PartitionSpec as P

TILE = 512
BAND = 4096


EPS = 1e-05


def from_everyone(x, axis):
    count = lax.axis_size(axis)
    return lax.all_to_all(jnp.broadcast_to(x[None], (count, *x.shape)), axis, 0, 0, tiled=True)


def taken_together(x, axis):
    everything = from_everyone(x, axis)
    return jnp.sum(everything, axis=0)


def in_one(arrays, axis):
    ends = [0]
    for a in arrays:
        ends.append(ends[-1] + a.size)
    running = taken_together(jnp.concatenate([a.ravel() for a in arrays]), axis)
    return tuple((running[b:e].reshape(a.shape) for a, b, e in zip(arrays, ends, ends[1:])))


def passed_along(x, axis, by):
    count = lax.axis_size(axis)
    pairs = [(i, i + by) for i in range(count) if 0 <= i + by < count]
    return lax.ppermute(x, axis, pairs)


def on_device(genotypes):
    present = (genotypes >= 0).astype(jnp.float32)
    dosage = genotypes * present
    counted, summed, squared = in_one(
        (jnp.sum(present, axis=0), jnp.sum(dosage, axis=0), jnp.sum(dosage * dosage, axis=0)),
        "samp",
    )
    average = summed / counted
    spread = squared / counted - average * average
    scaled = (present * (dosage - average) * lax.rsqrt(spread + EPS)).astype(jnp.bfloat16)
    col_norms = counted * spread / (spread + EPS)
    snp_dev = genotypes.shape[1]
    tiles_dev = snp_dev // TILE
    panels = (BAND - TILE + 2 * snp_dev - 1) // snp_dev - 1
    span_cols = (panels + 1) * snp_dev
    pieces = [scaled]
    norm_pieces = [col_norms]
    current = scaled
    current_norm = col_norms
    for distance in range(1, panels + 1):
        current = passed_along(current, "snp", -1)
        pieces.append(current)
        current_norm = passed_along(current_norm, "snp", -1)
        norm_pieces.append(current_norm)
    extended = jnp.concatenate(pieces, axis=1)
    device_pos = lax.axis_index("snp")
    far_norms = jnp.concatenate(norm_pieces)
    columns = device_pos * snp_dev + jnp.arange(span_cols, dtype=jnp.int32)
    inside = columns < lax.axis_size("snp") * snp_dev
    far_norms = jnp.where(inside, far_norms, 1.0)
    quarter = BAND // lax.axis_size("samp")
    partial_value = []
    for tile_pos in range(tiles_dev):
        row_block = scaled[:, tile_pos * TILE : (tile_pos + 1) * TILE]
        col_block = extended[:, tile_pos * TILE : tile_pos * TILE + BAND]
        partial_value.append(
            lax.dot_general(
                row_block, col_block, (((0,), (0,)), ((), ())), preferred_element_type=jnp.float32
            )
        )
    summed_tiles = jnp.concatenate(partial_value, axis=0)
    shares = lax.psum_scatter(
        summed_tiles.astype(jnp.bfloat16), "samp", scatter_dimension=1, tiled=True
    ).astype(jnp.float32)
    samp_pos = lax.axis_index("samp")
    results = []
    for tile_pos in range(tiles_dev):
        col_norm = lax.dynamic_slice_in_dim(
            far_norms, tile_pos * TILE + samp_pos * quarter, quarter, 0
        )
        row_norm = col_norms[tile_pos * TILE : (tile_pos + 1) * TILE]
        block_share = shares[tile_pos * TILE : (tile_pos + 1) * TILE]
        results.append(block_share / jnp.sqrt(row_norm[:, None] * col_norm[None, :]))
    return jnp.concatenate(results, axis=0)


def solution(mesh):
    in_specs = (P("samp", "snp"),)
    out_specs = P("snp", "samp")
    return jax.shard_map(
        on_device, mesh=mesh, in_specs=in_specs, out_specs=out_specs, check_vma=False
    )
```

profile of v0, /device:TPU:1, one launch (start us, length us, event | category | flops | bytes accessed | tf_op | source)
XLA Modules:
  0.0 402.3 jit_solution(11640251097026432255)
XLA Ops:
  6.5 0.0 reduce-scatter.2.cloned.1.call-start
  6.5 3.2 convert_reduce_fusion
  9.7 16.9 %all_to_all.6 = f32[4,1,3072]{2,1,0:T(1,128)S(1)} all-to-all(f32[4,1,3072]{2,1,0:T(1,128)S(1)} %broadcast_in_dim.5), channel_id=1, replica_groups=mesh['samp'=4,'snp'=64] {'samp'}, dimensions={0} | all-to-all | bytes 98304 | tf_op jit(solution)/shard_map/all_to_all | solution.py:15
  26.6 0.1 reduce_sum.39
  26.7 4.4 %constant_dynamic-update-slice_fusion.4 = (bf16[1024,5120]{1,0:T(8,128)(2,1)}, bf16[1024,1024]{1,0:T(8,128)(2,1)S(1)}) fusion(f32[1024]{0:T(1024)S(1)} %add_rsqrt_fusion, f32[1024]{0:T(1024)S(1)} %get-tuple-element.10, f32[1024,1024]{1,0:T(8,128)} %param.1), kind=kLoop, calls=%fused_computation.30 | loop fusion | flops 6291455 | bytes 8396800
  31.1 1.3 collective-permute-start
  32.4 47.0 %collective-permute-done = bf16[1024,1024]{1,0:T(8,128)(2,1)S(1)} collective-permute-done((bf16[1024,1024]{1,0:T(8,128)(2,1)S(1)}, bf16[1024,1024]{1,0:T(8,128)(2,1)S(1)}, u32[]{:S(2)}, u32[]{:S(2)}) %collective-permute-start) | collective-permute-done | bytes 2097184 | tf_op jit(solution)/shard_map/ppermute | solution.py:34
  79.4 1.3 collective-permute-start.1
  80.6 46.1 %collective-permute-done.1 = bf16[1024,1024]{1,0:T(8,128)(2,1)S(1)} collective-permute-done((bf16[1024,1024]{1,0:T(8,128)(2,1)S(1)}, bf16[1024,1024]{1,0:T(8,128)(2,1)S(1)}, u32[]{:S(2)}, u32[]{:S(2)}) %collective-permute-start.1) | collective-permute-done | bytes 2097184 | tf_op jit(solution)/shard_map/ppermute | solution.py:34
  126.7 1.3 collective-permute-start.2
  128.0 45.2 %collective-permute-done.2 = bf16[1024,1024]{1,0:T(8,128)(2,1)S(1)} collective-permute-done((bf16[1024,1024]{1,0:T(8,128)(2,1)S(1)}, bf16[1024,1024]{1,0:T(8,128)(2,1)S(1)}, u32[]{:S(2)}, u32[]{:S(2)}) %collective-permute-start.2) | collective-permute-done | bytes 2097184 | tf_op jit(solution)/shard_map/ppermute | solution.py:34
  173.3 1.3 collective-permute-start.3
  174.6 1.6 constant_dynamic-update-slice_fusion.3
  176.2 1.6 constant_dynamic-update-slice_fusion.2
  177.8 1.5 constant_dynamic-update-slice_fusion.1
  179.3 8.4 %fusion.13 = bf16[512,4096]{1,0:T(8,128)(2,1)} fusion(bf16[1024,1024]{1,0:T(8,128)(2,1)S(1)} %collective-permute-done.2, bf16[1024,1024]{1,0:T(8,128)(2,1)S(1)} %collective-permute-done.1, bf16[1024,1024]{1,0:T(8,128)(2,1)S(1)} %collective-permute-done, bf16[1024,1024]{1,0:T(8,128)(2,1)S(1)} %get-tuple-element.12), kind=kOutput, calls=%fused_computation.12 | convolution fusion | flops 4330618880 | bytes 13631488 | tf_op jit(solution)/shard_map/dot_general | solution.py:73
  187.8 34.0 %collective-permute-done.3 = bf16[1024,1024]{1,0:T(8,128)(2,1)S(1)} collective-permute-done((bf16[1024,1024]{1,0:T(8,128)(2,1)S(1)}, bf16[1024,1024]{1,0:T(8,128)(2,1)S(1)}, u32[]{:S(2)}, u32[]{:S(2)}) %collective-permute-start.3) | collective-permute-done | bytes 2097184 | tf_op jit(solution)/shard_map/ppermute | solution.py:34
  221.7 1.6 constant_dynamic-update-slice_fusion
  223.3 9.5 %fusion.10 = bf16[512,4096]{1,0:T(8,128)(2,1)} fusion(bf16[1024,5120]{1,0:T(8,128)(2,1)} %constant_dynamic-update-slice_fusion, bf16[1024,1024]{1,0:T(8,128)(2,1)S(1)} %get-tuple-element.12), kind=kOutput, calls=%fused_computation.11 | convolution fusion | flops 4297064448 | bytes 13631488 | tf_op jit(solution)/shard_map/dot_general | solution.py:73
  232.8 7.8 %pad_maximum_fusion = bf16[1024,4096]{1,0:T(8,128)(2,1)} fusion(bf16[512,4096]{1,0:T(8,128)(2,1)} %fusion.10, bf16[512,4096]{1,0:T(8,128)(2,1)} %fusion.13), kind=kLoop, calls=%fused_computation.10 | loop fusion | flops 16777216 | bytes 16777216 | tf_op jit(solution)/shard_map/concatenate | solution.py:77
  240.6 0.0 reduce-scatter.2.cloned.1.call-update
  240.7 1.3 collective-permute-start.4
  242.0 4.3 %collective-permute-done.4 = f32[1024]{0:T(1024)S(1)} collective-permute-done((f32[1024]{0:T(1024)S(1)}, f32[1024]{0:T(1024)S(1)}, u32[]{:S(2)}, u32[]{:S(2)}) %collective-permute-start.4) | collective-permute-done | bytes 4128 | tf_op jit(solution)/shard_map/ppermute | solution.py:34
  246.3 1.3 collective-permute-start.5
  247.6 4.6 %collective-permute-done.5 = f32[1024]{0:T(1024)S(1)} collective-permute-done((f32[1024]{0:T(1024)S(1)}, f32[1024]{0:T(1024)S(1)}, u32[]{:S(2)}, u32[]{:S(2)}) %collective-permute-start.5) | collective-permute-done | bytes 4128 | tf_op jit(solution)/shard_map/ppermute | solution.py:34
  252.2 1.3 collective-permute-start.6
  253.5 4.9 %collective-permute-done.6 = f32[1024]{0:T(1024)S(1)} collective-permute-done((f32[1024]{0:T(1024)S(1)}, f32[1024]{0:T(1024)S(1)}, u32[]{:S(2)}, u32[]{:S(2)}) %collective-permute-start.6) | collective-permute-done | bytes 4128 | tf_op jit(solution)/shard_map/ppermute | solution.py:34
  258.4 1.3 collective-permute-start.7
  259.7 5.2 %collective-permute-done.7 = f32[1024]{0:T(1024)S(1)} collective-permute-done((f32[1024]{0:T(1024)S(1)}, f32[1024]{0:T(1024)S(1)}, u32[]{:S(2)}, u32[]{:S(2)}) %collective-permute-start.7) | collective-permute-done | bytes 4128 | tf_op jit(solution)/shard_map/ppermute | solution.py:34
  264.8 0.1 fusion.22
  264.9 125.1 %reduce-scatter.2.cloned.1.call-done = bf16[1024,1024]{1,0:T(8,128)(2,1)} async-done(((bf16[1024,4096]{1,0:T(8,128)(2,1)}), bf16[1024,1024]{1,0:T(8,128)(2,1)}) %reduce-scatter.2.cloned.1.call-update) | async-done | bytes 2097168 | tf_op jit(solution)/shard_map/reduce_scatter | solution.py:78
  390.0 0.0 copy-start
  390.0 2.2 convert_element_type.12
  392.2 0.6 copy-done
  392.9 0.6 slice_multiply_fusion.1
  393.5 0.0 copy-start.1
  393.5 2.0 copy-done.1
  (11 shorter events, 0.1 us)
Async XLA Ops:
  6.5 383.5 %reduce-scatter.2.cloned.1.call-start = ((), (), s32[]{:S(2)}) async-start(), calls=%async_computation.2 | async-start | bytes 10485760 | tf_op jit(solution)/shard_map/reduce_scatter | solution.py:78
  31.1 48.2 %collective-permute-start = (bf16[1024,1024]{1,0:T(8,128)(2,1)S(1)}, bf16[1024,1024]{1,0:T(8,128)(2,1)S(1)}, u32[]{:S(2)}, u32[]{:S(2)}) collective-permute-start(bf16[1024,1024]{1,0:T(8,128)(2,1)S(1)} %get-tuple-element.12), channel_id=1, source_target_pairs={{1,0},{2,1},{3,2},{4,3},{5,4},{6,5},{7,6},{8,7},{9,8},{10,9},{11,1... | collective-permute-start | bytes 6291464 | tf_op jit(solution)/shard_map/ppermute | solution.py:34
  79.4 47.4 %collective-permute-start.1 = (bf16[1024,1024]{1,0:T(8,128)(2,1)S(1)}, bf16[1024,1024]{1,0:T(8,128)(2,1)S(1)}, u32[]{:S(2)}, u32[]{:S(2)}) collective-permute-start(bf16[1024,1024]{1,0:T(8,128)(2,1)S(1)} %collective-permute-done), channel_id=1, source_target_pairs={{1,0},{2,1},{3,2},{4,3},{5,4},{6,5},{7,6},{8,7},{9,8},{10,9},{11,1... | collective-permute-start | bytes 6291464 | tf_op jit(solution)/shard_map/ppermute | solution.py:34
  126.7 46.5 %collective-permute-start.2 = (bf16[1024,1024]{1,0:T(8,128)(2,1)S(1)}, bf16[1024,1024]{1,0:T(8,128)(2,1)S(1)}, u32[]{:S(2)}, u32[]{:S(2)}) collective-permute-start(bf16[1024,1024]{1,0:T(8,128)(2,1)S(1)} %collective-permute-done.1), channel_id=1, source_target_pairs={{1,0},{2,1},{3,2},{4,3},{5,4},{6,5},{7,6},{8,7},{9,8},{10,9},{11,1... | collective-permute-start | bytes 6291464 | tf_op jit(solution)/shard_map/ppermute | solution.py:34
  173.3 48.4 %collective-permute-start.3 = (bf16[1024,1024]{1,0:T(8,128)(2,1)S(1)}, bf16[1024,1024]{1,0:T(8,128)(2,1)S(1)}, u32[]{:S(2)}, u32[]{:S(2)}) collective-permute-start(bf16[1024,1024]{1,0:T(8,128)(2,1)S(1)} %collective-permute-done.2), channel_id=1, source_target_pairs={{1,0},{2,1},{3,2},{4,3},{5,4},{6,5},{7,6},{8,7},{9,8},{10,9},{11,1... | collective-permute-start | bytes 6291464 | tf_op jit(solution)/shard_map/ppermute | solution.py:34
  240.7 5.6 %collective-permute-start.4 = (f32[1024]{0:T(1024)S(1)}, f32[1024]{0:T(1024)S(1)}, u32[]{:S(2)}, u32[]{:S(2)}) collective-permute-start(f32[1024]{0:T(1024)S(1)} %get-tuple-element.9), channel_id=1, source_target_pairs={{1,0},{2,1},{3,2},{4,3},{5,4},{6,5},{7,6},{8,7},{9,8},{10,9},{11,1... | collective-permute-start | bytes 12296 | tf_op jit(solution)/shard_map/ppermute | solution.py:34
  246.3 5.9 %collective-permute-start.5 = (f32[1024]{0:T(1024)S(1)}, f32[1024]{0:T(1024)S(1)}, u32[]{:S(2)}, u32[]{:S(2)}) collective-permute-start(f32[1024]{0:T(1024)S(1)} %collective-permute-done.4), channel_id=1, source_target_pairs={{1,0},{2,1},{3,2},{4,3},{5,4},{6,5},{7,6},{8,7},{9,8},{10,9},{11,1... | collective-permute-start | bytes 12296 | tf_op jit(solution)/shard_map/ppermute | solution.py:34
  252.2 6.2 %collective-permute-start.6 = (f32[1024]{0:T(1024)S(1)}, f32[1024]{0:T(1024)S(1)}, u32[]{:S(2)}, u32[]{:S(2)}) collective-permute-start(f32[1024]{0:T(1024)S(1)} %collective-permute-done.5), channel_id=1, source_target_pairs={{1,0},{2,1},{3,2},{4,3},{5,4},{6,5},{7,6},{8,7},{9,8},{10,9},{11,1... | collective-permute-start | bytes 12296 | tf_op jit(solution)/shard_map/ppermute | solution.py:34
  258.4 6.5 %collective-permute-start.7 = (f32[1024]{0:T(1024)S(1)}, f32[1024]{0:T(1024)S(1)}, u32[]{:S(2)}, u32[]{:S(2)}) collective-permute-start(f32[1024]{0:T(1024)S(1)} %collective-permute-done.6), channel_id=1, source_target_pairs={{1,0},{2,1},{3,2},{4,3},{5,4},{6,5},{7,6},{8,7},{9,8},{10,9},{11,1... | collective-permute-start | bytes 12296 | tf_op jit(solution)/shard_map/ppermute | solution.py:34
  390.0 2.8 copy-start
  393.5 2.0 copy-start.1
Sparse Core Ops, SparseCore 0:
  240.8 149.2 reduce-scatter.1
where the time goes:
time: 403 us; the launch traced here: 402 us
  waiting for transfers between devices  316 us (78%)
  other arithmetic  18.3 us (5%)
  matrix products  17.9 us (4%)
  blocking collectives  16.9 us (4%)
  between operations  13.6 us (3%)
  starting transfers between devices  10.3 us (3%)
  local copies, waits for them, and re-layouts  9.1 us (2%)
    ppermute x8, waiting for transfers between devices, passed_along(): return lax.ppermute(x, axis, pairs)  191 us
    reduce_scatter x1, waiting for transfers between devices, on_device(): lax.psum_scatter(summed_tiles.astype(jnp.bfloat16), 'samp', scatter_dimen...  125 us
    dot_general x2, matrix products, on_device(): lax.dot_general(row_block, col_block, (((0,), (0,)), ((), ())), preferred...  17.9 us
    all_to_all x1, blocking collectives, from_everyone(): lax.all_to_all(jnp.broadcast_to(x[None], (count, *x.shape)), axis, 0, 0,...  16.9 us
    ppermute x8, starting transfers between devices, passed_along(): return lax.ppermute(x, axis, pairs)  10.3 us
  transfers between devices with their start and end apart: 9, of which 9 were waited for; matrix products, arithmetic and copies ran while one was open for 3% of the time, Pallas kernels for 0%

commit v1 on v0

v1 whole, which is shorter than its diff:
```python
import functools

import jax
import jax.numpy as jnp
from jax import lax
from jax.experimental import pallas as pl
from jax.experimental.pallas import tpu as pltpu
from jax.sharding import PartitionSpec as P

TILE = 512
BAND = 4096
EPS = 1e-05
CHUNK = 256
MESH = pl.DeviceIdType.MESH


def kernel(
    geno_hbm,
    out_hbm,
    geno,
    stats,
    ext,
    rows_t,
    acc,
    core_out,
    core_in,
    cross_out,
    cross_in,
    geno_sem,
    stats_send,
    stats_recv,
    back_send,
    ring_send,
    ext_recv,
    core_send,
    core_recv,
    cross_send,
    cross_recv,
    out_sem,
):
    samp = lax.axis_index("samp")
    snp = lax.axis_index("snp")
    n_snp = lax.axis_size("snp")
    half, core = samp // 2, samp % 2
    x = snp % 4
    row0 = snp - x
    has_prev = snp >= 4
    has_next = snp < n_snp - 4
    core_peer = (half * 2 + 1 - core, snp)
    cross_peer = ((1 - half) * 2 + core, snp)

    def remote(src, dst, send, recv, to):
        return pltpu.make_async_remote_copy(
            src_ref=src, dst_ref=dst, send_sem=send, recv_sem=recv, device_id=to, device_id_type=MESH
        )

    def geno_copy(c):
        return pltpu.make_async_copy(
            geno_hbm.at[:, pl.ds(c * CHUNK, CHUNK)], geno.at[c], geno_sem.at[c]
        )

    for c in range(4):
        geno_copy(c).start()

    barrier = pltpu.get_barrier_semaphore()
    for d in range(1, 4):
        pl.semaphore_signal(barrier, inc=1, device_id=((samp + d) % 4, snp), device_id_type=MESH)
        pl.semaphore_signal(barrier, inc=1, device_id=(samp, row0 + (x + d) % 4), device_id_type=MESH)

    @pl.when(has_prev)
    def _():
        pl.semaphore_signal(barrier, inc=1, device_id=(samp, snp - 4), device_id_type=MESH)

    @pl.when(has_next)
    def _():
        pl.semaphore_signal(barrier, inc=1, device_id=(samp, snp + 4), device_id_type=MESH)

    for c in range(4):
        geno_copy(c).wait()
        g = geno[c]
        dosage = jnp.maximum(g, 0.0)
        present = (g >= 0.0).astype(jnp.float32)
        cols = pl.ds(c * CHUNK, CHUNK)
        stats[samp, 0:1, cols] = jnp.sum(present, axis=0, keepdims=True)
        stats[samp, 1:2, cols] = jnp.sum(dosage, axis=0, keepdims=True)
        stats[samp, 2:3, cols] = jnp.sum(dosage * dosage, axis=0, keepdims=True)

    pl.semaphore_wait(
        barrier, 6 + has_prev.astype(jnp.int32) + has_next.astype(jnp.int32)
    )

    def stats_copy(d):
        return remote(
            stats.at[samp], stats.at[samp], stats_send.at[d - 1], stats_recv.at[samp], ((samp + d) % 4, snp)
        )

    for d in range(1, 4):
        stats_copy(d).start()

    @pl.when(jnp.logical_not(has_next))
    def _():
        for c in range(4):
            ext[16 + c] = jnp.zeros((1024, CHUNK), jnp.bfloat16)

    for d in range(1, 4):
        other = (samp + d) % 4
        remote(stats.at[other], stats.at[other], stats_send.at[d - 1], stats_recv.at[other], (other, snp)).wait_recv()

    def back_copy(c):
        return remote(ext.at[c], ext.at[16 + c], back_send.at[c], ext_recv.at[16 + c], (samp, snp - 4))

    def ring_copy(k, base, c):
        return remote(
            ext.at[base + c],
            ext.at[4 * k + c],
            ring_send.at[k - 1, c],
            ext_recv.at[4 * k + c],
            (samp, row0 + (x + 4 - k) % 4),
        )

    for c in range(4):
        cols = pl.ds(c * CHUNK, CHUNK)
        total = stats[0, 0:3, cols] + stats[1, 0:3, cols] + stats[2, 0:3, cols] + stats[3, 0:3, cols]
        counted, summed, squared = total[0:1], total[1:2], total[2:3]
        average = summed / counted
        spread = squared / counted - average * average
        col_norms = counted * spread / (spread + EPS)
        scale = lax.rsqrt(spread + EPS) * lax.rsqrt(col_norms)
        g = geno[c]
        scaled = jnp.where(g >= 0.0, (g - average) * scale, 0.0)
        ext[c] = scaled.astype(jnp.bfloat16)
        rows_t[pl.ds(c * CHUNK, CHUNK), :] = scaled.T.astype(jnp.bfloat16)

        @pl.when(has_prev & ((x < 3) | (c < 2)))
        def _():
            back_copy(c).start()

        for k in range(1, 4):

            @pl.when(x >= k)
            def _():
                ring_copy(k, 0, c).start()

    def chunk_of(i):
        j = i - 6
        b, kk = j // 3, j % 3
        k = jnp.where(kk == 0, 1, jnp.where(kk == 1, 3, 2))
        return jnp.where(i < 4, i, jnp.where(i < 6, 12 + i, 4 * k + b))

    def core_copy(u):
        return remote(core_out.at[u], core_in.at[u], core_send.at[u], core_recv.at[u], core_peer)

    def cross_copy(u):
        return remote(cross_out.at[u], cross_in.at[u], cross_send.at[u], cross_recv.at[u], cross_peer)

    def place(g, t):
        r = g - 2 * t
        q, m = r // 4, r % 4
        return (r >= 0) & (r < 16), q % 2 == core, q // 2, m

    def multiply(g):
        for t in range(2):
            valid, mine, h, m = place(g, t)

            @pl.when(valid)
            def _():
                u = (2 * t + h) * 4 + m
                part = jnp.dot(
                    rows_t[t * TILE : (t + 1) * TILE, :], ext[g], preferred_element_type=jnp.float32
                )

                @pl.when(mine)
                def _():
                    acc[u] = part

                @pl.when(jnp.logical_not(mine))
                def _():
                    core_out[u] = part.astype(jnp.bfloat16)
                    core_copy(u).start()

    def reduce(g):
        for t in range(2):
            valid, mine, h, m = place(g, t)

            @pl.when(valid & mine)
            def _():
                u = (2 * t + h) * 4 + m
                core_copy(u).wait_recv()

                @pl.when(h != half)
                def _():
                    v = t * 4 + m
                    cross_out[v] = (acc[u] + core_in[u].astype(jnp.float32)).astype(jnp.bfloat16)
                    cross_copy(v).start()

    def step(i, carry):
        @pl.when(i == 4)
        def _():
            for c in range(4):

                @pl.when(has_next & ((x < 3) | (c < 2)))
                def _():
                    back_copy(c).wait_recv()

                for k in range(1, 4):

                    @pl.when(x < k)
                    def _():
                        ring_copy(k, 16, c).start()

        @pl.when(i < 18)
        def _():
            g = chunk_of(i)

            @pl.when(i >= 6)
            def _():
                remote(ext.at[g], ext.at[g], ring_send.at[0, 0], ext_recv.at[g], core_peer).wait_recv()

            multiply(g)

        @pl.when(i > 0)
        def _():
            reduce(chunk_of(i - 1))

        return carry

    lax.fori_loop(0, 19, step, 0)

    def out_copy(v):
        t, m = v // 4, v % 4
        return pltpu.make_async_copy(
            acc.at[(2 * t + half) * 4 + m],
            out_hbm.at[pl.ds(t * TILE, TILE), pl.ds(pl.multiple_of(m * CHUNK, CHUNK), CHUNK)],
            out_sem.at[v],
        )

    def finish(v, carry):
        t, m = v // 4, v % 4
        u = (2 * t + half) * 4 + m
        cross_copy(v).wait_recv()
        acc[u] = acc[u] + core_in[u].astype(jnp.float32) + cross_in[v].astype(jnp.float32)
        out_copy(v).start()
        return carry

    lax.fori_loop(0, 8, finish, 0)

    for d in range(1, 4):
        stats_copy(d).wait_send()
    for c in range(4):

        @pl.when(has_prev & ((x < 3) | (c < 2)))
        def _():
            back_copy(c).wait_send()

        for k in range(1, 4):
            ring_copy(k, 0, c).wait_send()

    def drain_core(v, carry):
        t, hm = v // 8, v % 8
        h, m = hm // 4, hm % 4
        core_copy((2 * t + h) * 4 + m).wait_send()
        return carry

    lax.fori_loop(0, 16, drain_core, 0)

    def drain(v, carry):
        cross_copy(v).wait_send()
        out_copy(v).wait()
        return carry

    lax.fori_loop(0, 8, drain, 0)


def on_device(genotypes):
    samples, snps = genotypes.shape
    dma = pltpu.SemaphoreType.DMA
    return pl.pallas_call(
        kernel,
        out_shape=jax.ShapeDtypeStruct((snps, BAND // lax.axis_size("samp")), jnp.float32),
        in_specs=[pl.BlockSpec(memory_space=pl.ANY)],
        out_specs=pl.BlockSpec(memory_space=pl.ANY),
        scratch_shapes=[
            pltpu.VMEM((4, samples, CHUNK), jnp.float32),
            pltpu.VMEM((4, 8, snps), jnp.float32),
            pltpu.VMEM((20, samples, CHUNK), jnp.bfloat16),
            pltpu.VMEM((snps, samples), jnp.bfloat16),
            pltpu.VMEM((16, TILE, CHUNK), jnp.float32),
            pltpu.VMEM((16, TILE, CHUNK), jnp.bfloat16),
            pltpu.VMEM((16, TILE, CHUNK), jnp.bfloat16),
            pltpu.VMEM((8, TILE, CHUNK), jnp.bfloat16),
            pltpu.VMEM((8, TILE, CHUNK), jnp.bfloat16),
            dma((4,)),
            dma((3,)),
            dma((4,)),
            dma((4,)),
            dma((3, 4)),
            dma((20,)),
            dma((16,)),
            dma((16,)),
            dma((8,)),
            dma((8,)),
            dma((8,)),
        ],
        compiler_params=pltpu.CompilerParams(
            collective_id=0, has_side_effects=True, vmem_limit_bytes=60 * 2**20
        ),
        name="ld_band",
    )(genotypes)


def solution(mesh):
    return jax.shard_map(
        on_device, mesh=mesh, in_specs=(P("samp", "snp"),), out_specs=P("snp", "samp"), check_vma=False
    )
```

time: 403 us -> 166 us (0.41)
  the two profiles are of different devices: /device:TPU:1 before, /device:TPU:174 now
where the time goes in v1:
time: 166 us
  Pallas kernels  161 us (97%)
  local copies, waits for them, and re-layouts  4.79 us (3%)
    pallas_call x1, Pallas kernels, on_device(): pl.pallas_call(kernel, out_shape=jax.ShapeDtypeStruct((snps, BAND // lax....  161 us
    unnamed x1, local copies, waits for them, and re-layouts  4.79 us

profile of v1, /device:TPU:174, one launch (start us, length us, event | category | flops | bytes accessed | tf_op | source)
XLA Modules:
  0.0 166.1 jit_solution(5188041589344982849)
XLA Ops:
  0.0 161.3 %ld_band.1 = f32[1024,1024]{1,0:T(8,128)} custom-call(f32[1024,1024]{1,0:T(8,128)} %geno_hbm.1), custom_call_target="tpu_custom_call" | custom-call | tf_op jit(solution)/shard_map/ld_band/pallas_call | solution.py:277
  161.3 4.8 %copy.3 = f32[1024,1024]{1,0:T(8,128)} copy(f32[1024,1024]{1,0:T(8,128)} %ld_band.1) | data formatting | bytes 8388608

commit v2 on v1

--- a/solution.py
+++ b/solution.py
@@ -11,15 +11,36 @@
 BAND = 4096
 EPS = 1e-05
 CHUNK = 256
+MISSING = -4.0
+PRESENT = -3.0
 MESH = pl.DeviceIdType.MESH
+OWN = (0, 1, 2, 3)
+ORDER = (
+    OWN + (4, 5, 12, 6, 13, 7, 16, 17, 14, 8, 15, 9, 10, 11),
+    OWN + (4, 12, 13, 8, 14, 9, 16, 17, 15, 10, 11, 5, 6, 7),
+    OWN + (4, 5, 12, 6, 13, 7, 8, 9, 16, 17, 14, 15, 10, 11),
+    OWN + (16, 17, 4, 5, 8, 6, 9, 7, 12, 13, 14, 15, 10, 11),
+)
+PASS_AT = (4, 5, 7, 9)
+
+
+def look_up(i, values):
+    found = values[0]
+    for n, v in enumerate(values):
+        if n:
+            found = jnp.where(i == n, v, found)
+    return found
 
 
 def kernel(
     geno_hbm,
-    out_hbm,
+    out,
     geno,
     stats,
     ext,
+    affine,
+    own,
+    scratch,
     rows_t,
     acc,
     core_out,
@@ -31,12 +52,14 @@
     stats_recv,
     back_send,
     ring_send,
+    relay_send,
     ext_recv,
+    affine_send,
+    affine_recv,
     core_send,
     core_recv,
     cross_send,
     cross_recv,
-    out_sem,
 ):
     samp = lax.axis_index("samp")
     snp = lax.axis_index("snp")
@@ -85,9 +108,7 @@
         stats[samp, 1:2, cols] = jnp.sum(dosage, axis=0, keepdims=True)
         stats[samp, 2:3, cols] = jnp.sum(dosage * dosage, axis=0, keepdims=True)
 
-    pl.semaphore_wait(
-        barrier, 6 + has_prev.astype(jnp.int32) + has_next.astype(jnp.int32)
-    )
+    pl.semaphore_wait(barrier, 6 + has_prev.astype(jnp.int32) + has_next.astype(jnp.int32))
 
     def stats_copy(d):
         return remote(
@@ -97,26 +118,70 @@
     for d in range(1, 4):
         stats_copy(d).start()
 
+    def back_copy(c):
+        return remote(ext.at[c], ext.at[16 + c], back_send.at[c], ext_recv.at[16 + c], (samp, snp - 4))
+
+    def ring_to(k):
+        return (samp, row0 + (x + 4 - k) % 4)
+
+    def ring_copy(k, base, c):
+        return remote(
+            ext.at[base + c], ext.at[4 * k + c], ring_send.at[k - 1, c], ext_recv.at[4 * k + c], ring_to(k)
+        )
+
+    def affine_back():
+        return remote(affine.at[0], affine.at[4], affine_send.at[0], affine_recv.at[4], (samp, snp - 4))
+
+    def affine_ring(k, base):
+        return remote(affine.at[base], affine.at[k], affine_send.at[k], affine_recv.at[k], ring_to(k))
+
+    inner = (x == 1) | (x == 2)
+    late_near = (half == 0) & (x == 1)
+    late_far = (half == 1) & (x == 2)
+
+    def relay_to(k):
+        return (samp, jnp.where(k == 1, snp - 1, snp + 1))
+
+    def relay_copy(k, c):
+        return remote(
+            ext.at[4 * k + c], ext.at[8 + c], relay_send.at[4 * (k // 2) + c], ext_recv.at[8 + c], relay_to(k)
+        )
+
+    def affine_relay(k):
+        return remote(affine.at[k], affine.at[2], affine_send.at[4 + k // 2], affine_recv.at[2], relay_to(k))
+
+    def send_back(c):
+        @pl.when(has_prev & ((x < 3) | (c < 2)))
+        def _():
+            back_copy(c).start()
+
+    def send_ring(c):
+        @pl.when((x >= 1) if c == 0 else ((x >= 1) & jnp.logical_not(late_near)))
+        def _():
+            ring_copy(1, 0, c).start()
+
+        @pl.when(x >= 3)
+        def _():
+            ring_copy(3, 0, c).start()
+
+    for c in range(4):
+        cols = pl.ds(c * CHUNK, CHUNK)
+        g = geno[c]
+        middle = stats[samp, 1:2, cols] / stats[samp, 0:1, cols]
+        ext[c] = jnp.where(g >= 0.0, g - middle, MISSING).astype(jnp.bfloat16)
+        if c == 0:
+            send_back(0)
+            send_ring(0)
+
     @pl.when(jnp.logical_not(has_next))
     def _():
+        affine[4] = jnp.zeros((2, 1024), jnp.float32)
         for c in range(4):
             ext[16 + c] = jnp.zeros((1024, CHUNK), jnp.bfloat16)
 
     for d in range(1, 4):
         other = (samp + d) % 4
         remote(stats.at[other], stats.at[other], stats_send.at[d - 1], stats_recv.at[other], (other, snp)).wait_recv()
-
-    def back_copy(c):
-        return remote(ext.at[c], ext.at[16 + c], back_send.at[c], ext_recv.at[16 + c], (samp, snp - 4))
-
-    def ring_copy(k, base, c):
-        return remote(
-            ext.at[base + c],
-            ext.at[4 * k + c],
-            ring_send.at[k - 1, c],
-            ext_recv.at[4 * k + c],
-            (samp, row0 + (x + 4 - k) % 4),
-        )
 
     for c in range(4):
         cols = pl.ds(c * CHUNK, CHUNK)
@@ -126,26 +191,36 @@
         spread = squared / counted - average * average
         col_norms = counted * spread / (spread + EPS)
         scale = lax.rsqrt(spread + EPS) * lax.rsqrt(col_norms)
+        middle = stats[samp, 1:2, cols] / stats[samp, 0:1, cols]
+        affine[0, 0:1, cols] = scale
+        affine[0, 1:2, cols] = (middle - average) * scale
+
+    @pl.when(has_prev)
+    def _():
+        affine_back().start()
+
+    for k in (1, 3):
+
+        @pl.when(x >= k)
+        def _():
+            affine_ring(k, 0).start()
+
+    for c in range(1, 4):
+        send_back(c)
+        send_ring(c)
+
+    for c in range(4):
+        cols = pl.ds(c * CHUNK, CHUNK)
+        scale, shift = affine[0, 0:1, cols], affine[0, 1:2, cols]
+        middle = stats[samp, 1:2, cols] / stats[samp, 0:1, cols]
         g = geno[c]
-        scaled = jnp.where(g >= 0.0, (g - average) * scale, 0.0)
-        ext[c] = scaled.astype(jnp.bfloat16)
+        scaled = jnp.where(g >= 0.0, (g - middle) * scale + shift, 0.0)
+        own[c] = scaled.astype(jnp.bfloat16)
         rows_t[pl.ds(c * CHUNK, CHUNK), :] = scaled.T.astype(jnp.bfloat16)
 
-        @pl.when(has_prev & ((x < 3) | (c < 2)))
-        def _():
-            back_copy(c).start()
-
-        for k in range(1, 4):
-
-            @pl.when(x >= k)
-            def _():
-                ring_copy(k, 0, c).start()
-
     def chunk_of(i):
-        j = i - 6
-        b, kk = j // 3, j % 3
-        k = jnp.where(kk == 0, 1, jnp.where(kk == 1, 3, 2))
-        return jnp.where(i < 4, i, jnp.where(i < 6, 12 + i, 4 * k + b))
+        g = [look_up(i, order) for order in ORDER]
+        return jnp.where(half == 0, jnp.where(x == 0, g[1], g[0]), jnp.where(x == 3, g[3], g[2]))
 
     def core_copy(u):
         return remote(core_out.at[u], core_in.at[u], core_send.at[u], core_recv.at[u], core_peer)
@@ -158,7 +233,7 @@
         q, m = r // 4, r % 4
         return (r >= 0) & (r < 16), q % 2 == core, q // 2, m
 
-    def multiply(g):
+    def multiply(g, block):
         for t in range(2):
             valid, mine, h, m = place(g, t)
 
@@ -166,7 +241,7 @@
             def _():
                 u = (2 * t + h) * 4 + m
                 part = jnp.dot(
-                    rows_t[t * TILE : (t + 1) * TILE, :], ext[g], preferred_element_type=jnp.float32
+                    rows_t[t * TILE : (t + 1) * TILE, :], block[...], preferred_element_type=jnp.float32
                 )
 
                 @pl.when(mine)
@@ -194,29 +269,74 @@
                     cross_copy(v).start()
 
     def step(i, carry):
-        @pl.when(i == 4)
-        def _():
-            for c in range(4):
-
+        for c in range(4):
+
+            @pl.when(i == PASS_AT[c])
+            def _():
                 @pl.when(has_next & ((x < 3) | (c < 2)))
                 def _():
                     back_copy(c).wait_recv()
 
-                for k in range(1, 4):
-
-                    @pl.when(x < k)
+                @pl.when(x < 1)
+                def _():
+                    ring_copy(1, 16, c).start()
+
+                @pl.when((x < 3) if c == 3 else ((x < 3) & jnp.logical_not(late_far)))
+                def _():
+                    ring_copy(3, 16, c).start()
+
+                if c == 0:
+
+                    @pl.when(has_next)
                     def _():
-                        ring_copy(k, 16, c).start()
-
-        @pl.when(i < 18)
+                        affine_back().wait_recv()
+
+                    for k in (1, 3):
+
+                        @pl.when(x < k)
+                        def _():
+                            affine_ring(k, 4).start()
+
+        @pl.when(i < 4)
+        def _():
+            multiply(i, own.at[i])
+
+        @pl.when((i >= 4) & (i < 18))
         def _():
             g = chunk_of(i)
-
-            @pl.when(i >= 6)
+            k, b = g // 4, g % 4
+
+            @pl.when(k < 4)
             def _():
                 remote(ext.at[g], ext.at[g], ring_send.at[0, 0], ext_recv.at[g], core_peer).wait_recv()
 
-            multiply(g)
+                @pl.when(inner & (k != 2))
+                def _():
+                    relay_copy(k, b).start()
+
+                @pl.when(b == 0)
+                def _():
+                    affine_ring(k, 0).wait_recv()
+
+                    @pl.when(inner & (k != 2))
+                    def _():
+                        affine_relay(k).start()
+
+                @pl.when(late_near & (g == 7))
+                def _():
+                    for c in range(1, 4):
+                        ring_copy(1, 0, c).start()
+
+                @pl.when(late_far & (g == 13))
+                def _():
+                    for c in range(3):
+                        ring_copy(3, 16, c).start()
+
+            v = ext[g].astype(jnp.float32)
+            cols = pl.ds(pl.multiple_of(b * CHUNK, CHUNK), CHUNK)
+            scale, shift = affine[k, 0:1, cols], affine[k, 1:2, cols]
+            scratch[...] = jnp.where(v > PRESENT, v * scale + shift, 0.0).astype(jnp.bfloat16)
+            multiply(g, scratch)
 
         @pl.when(i > 0)
         def _():
@@ -225,21 +345,13 @@
         return carry
 
     lax.fori_loop(0, 19, step, 0)
-
-    def out_copy(v):
-        t, m = v // 4, v % 4
-        return pltpu.make_async_copy(
-            acc.at[(2 * t + half) * 4 + m],
-            out_hbm.at[pl.ds(t * TILE, TILE), pl.ds(pl.multiple_of(m * CHUNK, CHUNK), CHUNK)],
-            out_sem.at[v],
-        )
 
     def finish(v, carry):
         t, m = v // 4, v % 4
         u = (2 * t + half) * 4 + m
         cross_copy(v).wait_recv()
-        acc[u] = acc[u] + core_in[u].astype(jnp.float32) + cross_in[v].astype(jnp.float32)
-        out_copy(v).start()
+        rows, cols = pl.ds(pl.multiple_of(t * TILE, TILE), TILE), pl.ds(pl.multiple_of(m * CHUNK, CHUNK), CHUNK)
+        out[rows, cols] = acc[u] + core_in[u].astype(jnp.float32) + cross_in[v].astype(jnp.float32)
         return carry
 
     lax.fori_loop(0, 8, finish, 0)
@@ -252,8 +364,23 @@
         def _():
             back_copy(c).wait_send()
 
-        for k in range(1, 4):
+        for k in (1, 3):
             ring_copy(k, 0, c).wait_send()
+
+            @pl.when(inner)
+            def _():
+                relay_copy(k, c).wait_send()
+
+    @pl.when(has_prev)
+    def _():
+        affine_back().wait_send()
+
+    for k in (1, 3):
+        affine_ring(k, 0).wait_send()
+
+        @pl.when(inner)
+        def _():
+            affine_relay(k).wait_send()
 
     def drain_core(v, carry):
         t, hm = v // 8, v % 8
@@ -265,7 +392,6 @@
 
     def drain(v, carry):
         cross_copy(v).wait_send()
-        out_copy(v).wait()
         return carry
 
     lax.fori_loop(0, 8, drain, 0)
@@ -277,12 +403,15 @@
     return pl.pallas_call(
         kernel,
         out_shape=jax.ShapeDtypeStruct((snps, BAND // lax.axis_size("samp")), jnp.float32),
-        in_specs=[pl.BlockSpec(memory_space=pl.ANY)],
-        out_specs=pl.BlockSpec(memory_space=pl.ANY),
+        in_specs=[pl.BlockSpec(memory_space=pltpu.HBM)],
+        out_specs=pl.BlockSpec(memory_space=pltpu.VMEM),
         scratch_shapes=[
             pltpu.VMEM((4, samples, CHUNK), jnp.float32),
             pltpu.VMEM((4, 8, snps), jnp.float32),
             pltpu.VMEM((20, samples, CHUNK), jnp.bfloat16),
+            pltpu.VMEM((5, 2, snps), jnp.float32),
+            pltpu.VMEM((4, samples, CHUNK), jnp.bfloat16),
+            pltpu.VMEM((samples, CHUNK), jnp.bfloat16),
             pltpu.VMEM((snps, samples), jnp.bfloat16),
             pltpu.VMEM((16, TILE, CHUNK), jnp.float32),
             pltpu.VMEM((16, TILE, CHUNK), jnp.bfloat16),
@@ -294,15 +423,17 @@
             dma((4,)),
             dma((4,)),
             dma((3, 4)),
+            dma((8,)),
             dma((20,)),
+            dma((6,)),
+            dma((5,)),
             dma((16,)),
             dma((16,)),
             dma((8,)),
             dma((8,)),
-            dma((8,)),
         ],
         compiler_params=pltpu.CompilerParams(
-            collective_id=0, has_side_effects=True, vmem_limit_bytes=60 * 2**20
+            collective_id=0, has_side_effects=True, vmem_limit_bytes=47 * 2**20
         ),
         name="ld_band",
     )(genotypes)

time: 166 us -> 157 us (0.946)
  Pallas kernels: 161 us -> 155 us
  local copies, waits for them, and re-layouts: 4.79 us -> 2.02 us
    pallas_call x1, Pallas kernels: 161 us -> 155 us  [on_device(): pl.pallas_call(kernel, out_shape=jax.ShapeDtypeStruct((snps, BAND // lax....]
    unnamed x1, local copies, waits for them, and re-layouts: 4.79 us -> 2.02 us
where the time goes in v2:
time: 157 us
  Pallas kernels  155 us (99%)
  local copies, waits for them, and re-layouts  2.02 us (1%)
    pallas_call x1, Pallas kernels, on_device(): pl.pallas_call(kernel, out_shape=jax.ShapeDtypeStruct((snps, BAND // lax....  155 us

profile of v2, /device:TPU:174, one launch (start us, length us, event | category | flops | bytes accessed | tf_op | source)
XLA Modules:
  0.0 156.6 jit_solution(13098563602839340702)
XLA Ops:
  0.0 154.5 %ld_band.1 = f32[1024,1024]{1,0:T(8,128)S(1)} custom-call(f32[1024,1024]{1,0:T(8,128)} %geno_hbm.1), custom_call_target="tpu_custom_call" | custom-call | tf_op jit(solution)/shard_map/ld_band/pallas_call | solution.py:403
  154.6 2.0 %copy.3 = f32[1024,1024]{1,0:T(8,128)} copy(f32[1024,1024]{1,0:T(8,128)S(1)} %ld_band.1) | data formatting | bytes 8388608

commit v3 on v2

--- a/solution.py
+++ b/solution.py
@@ -16,12 +16,20 @@
 MESH = pl.DeviceIdType.MESH
 OWN = (0, 1, 2, 3)
 ORDER = (
-    OWN + (4, 5, 12, 6, 13, 7, 16, 17, 14, 8, 15, 9, 10, 11),
-    OWN + (4, 12, 13, 8, 14, 9, 16, 17, 15, 10, 11, 5, 6, 7),
-    OWN + (4, 5, 12, 6, 13, 7, 8, 9, 16, 17, 14, 15, 10, 11),
-    OWN + (16, 17, 4, 5, 8, 6, 9, 7, 12, 13, 14, 15, 10, 11),
+    (
+        OWN + (12, 16, 13, 17, 14, 8, 15, 9, 10, 11, 4, 5, 6, 7),
+        OWN + (4, 16, 5, 17, 6, 12, 7, 13, 8, 14, 9, 15, 10, 11),
+        OWN + (4, 16, 5, 12, 6, 13, 7, 17, 8, 14, 9, 15, 10, 11),
+        OWN + (16, 4, 17, 12, 5, 8, 13, 6, 9, 14, 7, 15, 10, 11),
+    ),
+    (
+        OWN + (4, 5, 6, 8, 7, 9, 16, 17, 12, 13, 14, 15, 10, 11),
+        OWN + (4, 5, 6, 16, 7, 17, 8, 9, 12, 13, 14, 15, 10, 11),
+        OWN + (4, 5, 12, 6, 13, 7, 8, 9, 16, 17, 14, 15, 10, 11),
+        OWN + (16, 4, 17, 5, 8, 6, 9, 7, 12, 13, 14, 15, 10, 11),
+    ),
 )
-PASS_AT = (4, 5, 7, 9)
+PASS_AT = (4, 6, 8, 10)
 
 
 def look_up(i, values):
@@ -135,7 +143,12 @@
     def affine_ring(k, base):
         return remote(affine.at[base], affine.at[k], affine_send.at[k], affine_recv.at[k], ring_to(k))
 
-    inner = (x == 1) | (x == 2)
+    def relays(k, c):
+        return ((k == 1) & (x >= 1)) | ((k == 3) & (x == 2))
+
+    def relays_affine(k):
+        return ((k == 1) & (x >= 1)) | ((k == 3) & (x == 2))
+
     late_near = (half == 0) & (x == 1)
     late_far = (half == 1) & (x == 2)
 
@@ -156,7 +169,7 @@
             back_copy(c).start()
 
     def send_ring(c):
-        @pl.when((x >= 1) if c == 0 else ((x >= 1) & jnp.logical_not(late_near)))
+        @pl.when((x >= 1) if c < 2 else ((x >= 1) & jnp.logical_not(late_near)))
         def _():
             ring_copy(1, 0, c).start()
 
@@ -205,6 +218,7 @@
         def _():
             affine_ring(k, 0).start()
 
+
     for c in range(1, 4):
         send_back(c)
         send_ring(c)
@@ -219,8 +233,8 @@
         rows_t[pl.ds(c * CHUNK, CHUNK), :] = scaled.T.astype(jnp.bfloat16)
 
     def chunk_of(i):
-        g = [look_up(i, order) for order in ORDER]
-        return jnp.where(half == 0, jnp.where(x == 0, g[1], g[0]), jnp.where(x == 3, g[3], g[2]))
+        g = [look_up(x, [look_up(i, order) for order in orders]) for orders in ORDER]
+        return jnp.where(half == 0, g[0], g[1])
 
     def core_copy(u):
         return remote(core_out.at[u], core_in.at[u], core_send.at[u], core_recv.at[u], core_peer)
@@ -310,7 +324,7 @@
             def _():
                 remote(ext.at[g], ext.at[g], ring_send.at[0, 0], ext_recv.at[g], core_peer).wait_recv()
 
-                @pl.when(inner & (k != 2))
+                @pl.when(relays(k, b))
                 def _():
                     relay_copy(k, b).start()
 
@@ -318,13 +332,13 @@
                 def _():
                     affine_ring(k, 0).wait_recv()
 
-                    @pl.when(inner & (k != 2))
+                    @pl.when(relays_affine(k))
                     def _():
                         affine_relay(k).start()
 
                 @pl.when(late_near & (g == 7))
                 def _():
-                    for c in range(1, 4):
+                    for c in range(2, 4):
                         ring_copy(1, 0, c).start()
 
                 @pl.when(late_far & (g == 13))
@@ -367,9 +381,10 @@
         for k in (1, 3):
             ring_copy(k, 0, c).wait_send()
 
-            @pl.when(inner)
+            @pl.when(relays(k, c))
             def _():
                 relay_copy(k, c).wait_send()
+
 
     @pl.when(has_prev)
     def _():
@@ -378,9 +393,10 @@
     for k in (1, 3):
         affine_ring(k, 0).wait_send()
 
-        @pl.when(inner)
+        @pl.when(relays_affine(k))
         def _():
             affine_relay(k).wait_send()
+
 
     def drain_core(v, carry):
         t, hm = v // 8, v % 8

time: 157 us -> 152 us (0.968)
  the two profiles are of different devices: /device:TPU:174 before, /device:TPU:28 now
where the time goes in v3:
time: 152 us
  Pallas kernels  150 us (99%)
  local copies, waits for them, and re-layouts  2.02 us (1%)
    pallas_call x1, Pallas kernels, on_device(): pl.pallas_call(kernel, out_shape=jax.ShapeDtypeStruct((snps, BAND // lax....  150 us

profile of v3, /device:TPU:28, one launch (start us, length us, event | category | flops | bytes accessed | tf_op | source)
XLA Modules:
  0.0 152.0 jit_solution(3726493537147691220)
XLA Ops:
  0.0 150.0 %ld_band.1 = f32[1024,1024]{1,0:T(8,128)S(1)} custom-call(f32[1024,1024]{1,0:T(8,128)} %geno_hbm.1), custom_call_target="tpu_custom_call" | custom-call | tf_op jit(solution)/shard_map/ld_band/pallas_call | solution.py:419
  150.0 2.0 %copy.3 = f32[1024,1024]{1,0:T(8,128)} copy(f32[1024,1024]{1,0:T(8,128)S(1)} %ld_band.1) | data formatting | bytes 8388608

commit v4 on v3

--- a/solution.py
+++ b/solution.py
@@ -242,6 +242,15 @@
     def cross_copy(u):
         return remote(cross_out.at[u], cross_in.at[u], cross_send.at[u], cross_recv.at[u], cross_peer)
 
+    sends_mirror = (half == 1) & (core == 0)
+    has_mirror = (half == 0) & (core == 0)
+    upper = pl.ds(0, TILE // 2)
+
+    def upper_copy(u):
+        return remote(
+            cross_out.at[u, upper], cross_in.at[u, upper], cross_send.at[u], cross_recv.at[u], cross_peer
+        )
+
     def place(g, t):
         r = g - 2 * t
         q, m = r // 4, r % 4
@@ -280,7 +289,14 @@
                 def _():
                     v = t * 4 + m
                     cross_out[v] = (acc[u] + core_in[u].astype(jnp.float32)).astype(jnp.bfloat16)
-                    cross_copy(v).start()
+
+                    @pl.when(sends_mirror & (m == 0))
+                    def _():
+                        upper_copy(v).start()
+
+                    @pl.when(jnp.logical_not(sends_mirror & (m == 0)))
+                    def _():
+                        cross_copy(v).start()
 
     def step(i, carry):
         for c in range(4):
@@ -363,9 +379,28 @@
     def finish(v, carry):
         t, m = v // 4, v % 4
         u = (2 * t + half) * 4 + m
-        cross_copy(v).wait_recv()
-        rows, cols = pl.ds(pl.multiple_of(t * TILE, TILE), TILE), pl.ds(pl.multiple_of(m * CHUNK, CHUNK), CHUNK)
-        out[rows, cols] = acc[u] + core_in[u].astype(jnp.float32) + cross_in[v].astype(jnp.float32)
+        cols = pl.ds(pl.multiple_of(m * CHUNK, CHUNK), CHUNK)
+
+        @pl.when(has_mirror & (m == 0))
+        def _():
+            upper_copy(v).wait_recv()
+            rows = pl.ds(pl.multiple_of(t * TILE, TILE), TILE // 2)
+            out[rows, cols] = (
+                acc[u, upper] + core_in[u, upper].astype(jnp.float32) + cross_in[v, upper].astype(jnp.float32)
+            )
+
+        @pl.when(jnp.logical_not(has_mirror & (m == 0)))
+        def _():
+            cross_copy(v).wait_recv()
+            rows = pl.ds(pl.multiple_of(t * TILE, TILE), TILE)
+            out[rows, cols] = acc[u] + core_in[u].astype(jnp.float32) + cross_in[v].astype(jnp.float32)
+
+        @pl.when(has_mirror & (m == 1))
+        def _():
+            rows = pl.ds(pl.multiple_of(t * TILE, TILE), TILE // 2)
+            low = pl.ds(pl.multiple_of(t * TILE + TILE // 2, TILE // 2), TILE // 2)
+            out[low, pl.ds(0, CHUNK)] = out[rows, pl.ds(CHUNK, CHUNK)].T
+
         return carry
 
     lax.fori_loop(0, 8, finish, 0)
@@ -407,7 +442,14 @@
     lax.fori_loop(0, 16, drain_core, 0)
 
     def drain(v, carry):
-        cross_copy(v).wait_send()
+        @pl.when(sends_mirror & (v % 4 == 0))
+        def _():
+            upper_copy(v).wait_send()
+
+        @pl.when(jnp.logical_not(sends_mirror & (v % 4 == 0)))
+        def _():
+            cross_copy(v).wait_send()
+
         return carry
 
     lax.fori_loop(0, 8, drain, 0)

time: 152 us -> 150 us (0.987)
  the two profiles are of different devices: /device:TPU:28 before, /device:TPU:174 now
where the time goes in v4:
time: 150 us; the launch traced here: 147 us
  Pallas kernels  145 us (97%)
  local copies, waits for them, and re-layouts  2.02 us (1%)
    pallas_call x1, Pallas kernels, on_device(): pl.pallas_call(kernel, out_shape=jax.ShapeDtypeStruct((snps, BAND // lax....  145 us

profile of v4, /device:TPU:174, one launch (start us, length us, event | category | flops | bytes accessed | tf_op | source)
XLA Modules:
  0.0 147.0 jit_solution(9709517933154709144)
XLA Ops:
  0.0 145.0 %ld_band.1 = f32[1024,1024]{1,0:T(8,128)S(1)} custom-call(f32[1024,1024]{1,0:T(8,128)} %geno_hbm.1), custom_call_target="tpu_custom_call" | custom-call | tf_op jit(solution)/shard_map/ld_band/pallas_call | solution.py:461
  145.0 2.0 %copy.3 = f32[1024,1024]{1,0:T(8,128)} copy(f32[1024,1024]{1,0:T(8,128)S(1)} %ld_band.1) | data formatting | bytes 8388608
